TPU v7x, 512 devices: a whole 4x8x8 slice. The times are simulated.
512 devices in a mesh: elem: 32 (over z, x), lev: 16 (over y, core).
Axes of the slice: x: 4, y: 8, z: 8, core: 2. Of those that a mesh axis runs over, the one named last changes fastest.
Arguments:
- cloud_state: float32 [4096, 8, 4096], P(('elem', 'lev')), may hold values from -6 to 6
- substeps: int32 [4096], P('elem'), may hold values from 4 to 16
- element_links: int32 [1024, 4], P('elem'), may hold values from 0 to 1023, as said below
- host_state: float32 [4, 64, 16384], P(None, 'lev', 'elem'), may hold values from -6 to 6
- wind_field: float32 [2, 64, 16384], P(None, 'lev', 'elem'), may hold values from -3 to 3
- node_mass: float32 [16384], P('elem'), may hold values from 0.25 to 4
- field_coupling: float32 [8, 8], replicated, may hold values from -2 to 2
- force_map: float32 [8, 4], replicated, may hold values from -3 to 3
- feedback_map: float32 [4, 8], replicated, may hold values from -5 to 5
Outputs:
- cloud_new: float32 [4096, 8, 4096], P(('elem', 'lev'))
- host_new: float32 [4, 64, 16384], P(None, 'lev', 'elem')
Inputs may be any that keep to these rules, and one draw needn't show every extreme that they name: `element_links`: the 1024 elements form a doubly periodic grid of 16 rows in which each index of elem holds two neighbouring grid columns, all rows, in some order; element e lies on index e // 32 of elem. Entries 0 to 3 of row e give the global index of the element to the left, right, below and above element e. An element's right edge meets its right neighbour's left edge node for node (same j), its upper edge its upper neighbour's lower edge (same i). The left neighbour lies on the same index of elem or the one before it (cyclically), the right one on the same or the one after it, the lower and upper ones on the same index.
All inputs are finite; a program needn't handle non-finite values.
Results may differ from a plain program's by a relative error of at most 0.0003.
Values sent between devices are 32-bit elements; how exact they have to be, the bound alone decides.
No kernel may reach another device: no remote copies, remote signals or barrier semaphores. Data moves between devices by JAX's collectives and lax.ppermute only.
A program may use at most 64 MiB of HBM per device.

v0:
```python
import jax
import jax.numpy as jnp
import numpy as np
from jax import lax
from jax.sharding import PartitionSpec as P

CRM_X = 64
lateral_mix = 0.2
vertical_mix = 0.2
cloud_step = 0.1
host_step = 0.1
host_mix = 0.2
highest = lax.Precision.HIGHEST


def padded_2(cells, sides, width, closed):
    for axis, dim in sides:
        count = lax.axis_size(axis)
        ends = count if closed else count - 1
        head = lax.slice_in_dim(cells, 0, width, axis=dim)
        tail = lax.slice_in_dim(cells, cells.shape[dim] - width, cells.shape[dim], axis=dim)
        cells = jnp.concatenate(
            [
                lax.ppermute(tail, axis, [(i, (i + 1) % count) for i in range(ends)]),
                cells,
                lax.ppermute(head, axis, [((i + 1) % count, i) for i in range(ends)]),
            ],
            axis=dim,
        )
    return cells


def gll_derivative():
    points = np.array([-1.0, -1.0 / np.sqrt(5.0), 1.0 / np.sqrt(5.0), 1.0])
    weights = np.array(
        [
            1.0 / np.prod([points[index] - points[other] for other in range(4) if other != index])
            for index in range(4)
        ]
    )
    matrix = np.zeros((4, 4))
    for target in range(4):
        for source in range(4):
            if target != source:
                matrix[target, source] = (
                    weights[source] / weights[target] / (points[target] - points[source])
                )
        matrix[target, target] = -np.sum(matrix[target])
    return matrix


def advance_clouds(cloud, driving, counts, coupling):
    n_rows, n_fields, n_cells = cloud.shape
    cell_width = CRM_X
    n_levels = n_cells // cell_width
    spread = jnp.repeat(driving, cell_width, axis=2)

    def one_step(stepno, current):
        extended = jnp.pad(current, ((0, 0), (0, 0), (cell_width, cell_width)))
        upper_cells = extended[:, :, 2 * cell_width :]
        lower_cells = extended[:, :, : -2 * cell_width]
        shaped = current.reshape(n_rows, n_fields, n_levels, cell_width)
        eastward = jnp.roll(shaped, -1, axis=3).reshape(current.shape)
        westward = jnp.roll(shaped, 1, axis=3).reshape(current.shape)
        reaction = jnp.tanh(jnp.einsum("gf,nfc->ngc", coupling, current, precision=highest))
        update = (
            current
            + (
                lateral_mix * (eastward + westward - 2.0 * current)
                + vertical_mix * (upper_cells + lower_cells - 2.0 * current)
            )
            + cloud_step * (reaction + spread)
        )
        return jnp.where((stepno < counts)[:, None, None], update, current)

    return lax.fori_loop(0, jnp.max(counts), one_step, cloud)


def edge_tables(element_links, n_nodes):
    elem_dev = n_nodes // 16
    quarter = 4 * elem_dev
    my_index = lax.axis_index("elem")
    node_ids = jnp.arange(n_nodes, dtype=jnp.int32)
    elem_of = node_ids // 16
    row_of = node_ids // 4 % 4
    col_of = node_ids % 4
    edge_ids = jnp.arange(2 * quarter, dtype=jnp.int32)
    inner = edge_ids % quarter
    edge_node = inner // 4 * 16 + inner % 4 * 4 + jnp.where(edge_ids < quarter, 0, 3)
    picker = (node_ids[:, None] == edge_node[None, :]).astype(jnp.float32)
    left_ids = element_links[:, 0][elem_of]
    right_ids = element_links[:, 1][elem_of]
    left_base = jnp.where(left_ids // elem_dev == my_index, 2 * quarter, 0)
    right_base = jnp.where(right_ids // elem_dev == my_index, 2 * quarter, 4 * quarter)
    left_source = left_base + quarter + left_ids % elem_dev * 4 + row_of
    right_source = right_base + right_ids % elem_dev * 4 + row_of
    side_source = jnp.where(col_of == 0, left_source, jnp.where(col_of == 3, right_source, -1))
    sideways = (jnp.arange(6 * quarter, dtype=jnp.int32)[:, None] == side_source[None, :]).astype(
        jnp.float32
    )
    lower_ids = element_links[:, 2][elem_of] % elem_dev
    upper_ids = element_links[:, 3][elem_of] % elem_dev
    lower_source = lower_ids * 16 + 12 + col_of
    upper_source = upper_ids * 16 + col_of
    vert_source = jnp.where(row_of == 0, lower_source, jnp.where(row_of == 3, upper_source, -1))
    vertical = (node_ids[:, None] == vert_source[None, :]).astype(jnp.float32)
    return (picker, sideways, vertical)


def edge_sum(quantity, tables):
    picker, sideways, vertical = tables
    lead, levels, n_nodes = quantity.shape
    flat = quantity.reshape(lead * levels, n_nodes)
    edges = jnp.dot(flat, picker, precision=highest).reshape(lead, levels, picker.shape[1])
    with_peers = padded_2(edges, (("elem", 2),), picker.shape[1], True)
    first = flat + jnp.dot(
        with_peers.reshape(lead * levels, sideways.shape[0]), sideways, precision=highest
    )
    second = first + jnp.dot(first, vertical, precision=highest)
    return second.reshape(lead, levels, n_nodes)


def shards(
    cloud_state,
    substeps,
    element_links,
    host_state,
    wind_field,
    node_mass,
    field_coupling,
    force_map,
    feedback_map,
):
    own_rows, n_fields, n_cells = cloud_state.shape
    n_vars, lev_dev, n_nodes = host_state.shape
    n_cols = substeps.shape[0]
    elem_dev = n_nodes // 16
    cell_width = CRM_X
    lev_at = lax.axis_index("lev")
    node_ids = jnp.arange(n_nodes)
    column_of_node = node_ids // 16 * 4 + node_ids // 4 % 4 // 2 * 2 + node_ids % 4 // 2
    member = (column_of_node[:, None] == jnp.arange(n_cols)[None, :]).astype(jnp.float32)
    pooling = 0.25 * member
    host_flat = host_state.reshape(n_vars * lev_dev, n_nodes)
    host_columns = (
        jnp.dot(host_flat, pooling, precision=highest)
        .reshape(n_vars, lev_dev, n_cols)
        .transpose(2, 0, 1)
    )
    every_host = lax.all_gather(host_columns, "lev", axis=2, tiled=True)
    whole_host = lax.dynamic_slice_in_dim(every_host, lev_at * own_rows, own_rows, 0)
    driving = jnp.einsum("fv,nvl->nfl", force_map, whole_host, precision=highest)
    own_counts = lax.dynamic_slice_in_dim(substeps, lev_at * own_rows, own_rows, 0)
    cloud_new = advance_clouds(cloud_state, driving, own_counts, field_coupling)
    n_levels = n_cells // cell_width
    change = (
        (cloud_new - cloud_state).reshape(own_rows, n_fields, n_levels, cell_width).mean(axis=3)
    )
    every_change = lax.all_gather(change, "lev", axis=0, tiled=True)
    level_change = lax.dynamic_slice_in_dim(every_change, lev_at * lev_dev, lev_dev, 2)
    column_tendency = jnp.einsum("vf,nfl->vln", feedback_map, level_change, precision=highest)
    physics = jnp.dot(
        column_tendency.reshape(n_vars * lev_dev, n_cols), member.T, precision=highest
    ).reshape(n_vars, lev_dev, n_nodes)
    derivative = gll_derivative()
    kron_x = jnp.asarray(np.kron(np.eye(elem_dev * 4), derivative).T, jnp.float32)
    kron_y = jnp.asarray(np.kron(np.eye(elem_dev), np.kron(derivative, np.eye(4))).T, jnp.float32)

    def tendency(field):
        flat = field.reshape(n_vars * lev_dev, n_nodes)
        along_x = jnp.dot(flat, kron_x, precision=highest).reshape(field.shape)
        along_y = jnp.dot(flat, kron_y, precision=highest).reshape(field.shape)
        padded = padded_2(field, (("lev", 1),), 1, False)
        return (
            -(wind_field[0] * along_x + wind_field[1] * along_y)
            + host_mix * (padded[:, 2:] + padded[:, :-2] - 2.0 * field)
            + physics
        )

    tables = edge_tables(element_links, n_nodes)
    mass_total = edge_sum(node_mass.reshape(1, 1, n_nodes), tables)

    def smooth(values):
        return edge_sum(node_mass * values, tables) / mass_total

    first_section = smooth(host_state + host_step * tendency(host_state))
    second_section = smooth(
        0.75 * host_state + 0.25 * (first_section + host_step * tendency(first_section))
    )
    host_new = smooth(
        host_state / 3.0 + 2.0 / 3.0 * (second_section + host_step * tendency(second_section))
    )
    return (cloud_new, host_new)


def solution(mesh):
    placed = (
        P(("elem", "lev"), None, None),
        P("elem"),
        P("elem", None),
        P(None, "lev", "elem"),
        P(None, "lev", "elem"),
        P("elem"),
        P(),
        P(),
        P(),
    )
    return jax.shard_map(
        shards,
        mesh=mesh,
        in_specs=placed,
        out_specs=(P(("elem", "lev"), None, None), P(None, "lev", "elem")),
        check_vma=False,
    )
```

profile of v0, /device:TPU:230, one launch (start us, length us, event | category | flops | bytes accessed | tf_op | source)
XLA Modules:
  0.0 390.2 jit_solution(18212692638045972472)
XLA Ops:
  0.7 1.0 convolution_bitcast_fusion.4
  1.7 5.4 %collective-permute-start.4 = (f32[1,1,256]{2,1,0:T(1,128)S(1)}, f32[1,1,256]{2,1,0:T(1,128)S(1)}, u32[]{:S(2)}, u32[]{:S(2)}) collective-permute-start(f32[1,1,256]{2,1,0:T(1,128)S(1)} %convolution_bitcast_fusion.4), channel_id=1, source_target_pairs={{0,16},{16,32},{32,48},{48,64},{64,80},{80,96},{96,112},{112,128},... | collective-permute-start | bytes 3080 | tf_op jit(solution)/shard_map/ppermute | solution.py:24
  7.1 1.9 collective-permute-start.5
  9.9 1.9 collective-permute-start
  11.8 2.4 collective-permute-start.1
  14.3 2.1 fusion.138
  16.4 2.1 fusion.137
  18.4 2.1 fusion.136
  20.6 1.9 fusion.139
  24.1 2.1 fusion.134
  26.2 2.1 fusion.133
  28.3 2.1 fusion.135
  30.8 15.3 %all_gather.6 = f32[128,4,64]{0,1,2:T(4,128)S(1)} all-gather(f32[128,4,4]{0,1,2:T(4,128)S(1)} %bitcast.238), channel_id=1, replica_groups=mesh['elem'=32,'lev'=16] {'lev'}, dimensions={2}, use_global_device_ids=true | all-gather | bytes 139264 | tf_op jit(solution)/shard_map/all_gather | solution.py:150
  46.3 1.5 fusion.127
  48.0 68.8 %while.13 = (s32[]{:T(128)}, f32[8,8,4096]{2,1,0:T(8,128)S(1)}, s32[]{:T(128)}, s32[8]{0:T(128)S(1)}, f32[8,8]{1,0:T(8,128)S(1)}, /*index=5*/f32[8,8,64]{2,1,0:T(8,128)S(1)}, s32[]{:T(128)}) while((s32[]{:T(128)}, f32[8,8,4096]{2,1,0:T(8,128)S(1)}, s32[]{:T(128)}, s32[8]{0:T(128)S(1)}, f32[8,8]{1,0:T(8,128)S(1)}, ...), condition=%wide.region_2.3_spmd.clone, body=%wide.region_1.2_spmd.clone.sunk | while | flops 28835848 | bytes 22041208 | solution.py:76
  51.1 1.2 maximum_add_fusion.2
  52.3 1.6 add.880
  54.5 1.6 reshape.997
  56.1 3.2 fusion.176
  62.5 1.2 maximum_add_fusion.2
  63.6 1.6 add.880
  65.9 1.6 reshape.997
  67.5 3.2 fusion.176
  73.8 1.2 maximum_add_fusion.2
  75.0 1.6 add.880
  77.2 1.6 reshape.997
  78.8 3.2 fusion.176
  85.1 1.2 maximum_add_fusion.2
  86.3 1.6 add.880
  88.6 1.6 reshape.997
  90.2 3.2 fusion.176
  96.5 1.2 maximum_add_fusion.2
  97.6 1.6 add.880
  99.9 1.6 reshape.997
  101.5 3.2 fusion.176
  107.8 1.2 maximum_add_fusion.2
  109.0 1.6 add.880
  111.2 1.6 reshape.997
  112.9 3.2 fusion.176
  116.8 1.8 sub.95
  118.6 2.2 reshape.403
  120.8 2.3 reduce_sum.9
  123.1 17.1 %all_gather.7 = f32[128,8,64]{2,1,0:T(8,128)S(1)} all-gather(f32[8,8,64]{2,1,0:T(8,128)S(1)} %broadcast_multiply_fusion), channel_id=1, replica_groups=mesh['elem'=32,'lev'=16] {'lev'}, dimensions={0}, use_global_device_ids=true | all-gather | bytes 278528 | tf_op jit(solution)/shard_map/all_gather | solution.py:159
  141.9 4.2 %select_select_fusion.3 = s32[512,1]{0,1:T(1,128)S(1)} fusion(s32[]{:T(128)} %bitcast.40, s32[]{:T(128)} %bitcast.41, s32[]{:T(128)} %bitcast.42, s32[]{:T(128)} %bitcast.43, s32[]{:T(128)} %bitcast.44, s32[]{:T(128)} %bitcast.46, s32[]{:T(128)} %bitcast.45), kind=kLoop, calls=%fused_computation.216 | loop fusion | flops 11776 | bytes 2076 | tf_op jit(solution)/shard_map/gather | solution.py:91
  146.1 4.4 %select_select_fusion.2 = s32[512,1]{0,1:T(1,128)S(1)} fusion(s32[]{:T(128)} %bitcast.73, s32[]{:T(128)} %bitcast.74, s32[]{:T(128)} %bitcast.75, s32[]{:T(128)} %bitcast.76, s32[]{:T(128)} %bitcast.77, s32[]{:T(128)} %bitcast.79, s32[]{:T(128)} %bitcast.78), kind=kLoop, calls=%fused_computation.215 | loop fusion | flops 11776 | bytes 2076 | tf_op jit(solution)/shard_map/gather | solution.py:92
  150.4 4.4 %select_select_fusion.1 = s32[512,1]{0,1:T(1,128)S(1)} fusion(s32[]{:T(128)} %bitcast.106, s32[]{:T(128)} %bitcast.107, s32[]{:T(128)} %bitcast.108, s32[]{:T(128)} %bitcast.109, s32[]{:T(128)} %bitcast.110, s32[]{:T(128)} %bitcast.112, s32[]{:T(128)} %bitcast.111), kind=kLoop, calls=%fused_computation.214 | loop fusion | flops 11776 | bytes 2076 | tf_op jit(solution)/shard_map/gather | solution.py:101
  154.9 4.5 %select_select_fusion = s32[512,1]{0,1:T(1,128)S(1)} fusion(s32[]{:T(128)} %bitcast.139, s32[]{:T(128)} %bitcast.140, s32[]{:T(128)} %bitcast.141, s32[]{:T(128)} %bitcast.142, s32[]{:T(128)} %bitcast.143, s32[]{:T(128)} %bitcast.145, s32[]{:T(128)} %bitcast.144), kind=kLoop, calls=%fused_computation.213 | loop fusion | flops 11776 | bytes 2076 | tf_op jit(solution)/shard_map/gather | solution.py:102
  159.3 30.8 %fusion.104 = s32[512]{0:T(512)S(1)} fusion(pred[512]{0:T(512)(128)(4,1)S(1)} %compare_reduce_fusion, pred[512]{0:T(512)(128)(4,1)S(1)} %compare_reduce_fusion.1, pred[512]{0:T(512)(128)(4,1)S(1)} %compare_reduce_fusion.2, pred[512]{0:T(512)(128)(4,1)S(1)} %compare_reduce_fusion.3, pred[512]{0:T(512)(128)(4,1)S(1)} %compare_reduce_fusion.4, ...), kind=kLoop, calls=%fused_computation.204 | loop fusion | flops 53248 | bytes 19144 | tf_op jit(solution)/shard_map/jit(_where)/select_n | solution.py:105
  190.2 31.2 %fusion.94 = s32[512]{0:T(512)S(1)} fusion(pred[512]{0:T(512)(128)(4,1)S(1)} %compare_reduce_fusion, pred[512]{0:T(512)(128)(4,1)S(1)} %compare_reduce_fusion.1, pred[512]{0:T(512)(128)(4,1)S(1)} %compare_reduce_fusion.2, pred[512]{0:T(512)(128)(4,1)S(1)} %compare_reduce_fusion.3, pred[512]{0:T(512)(128)(4,1)S(1)} %compare_reduce_fusion.4, ...), kind=kLoop, calls=%fused_computation.194 | loop fusion | flops 64512 | bytes 19148 | tf_op jit(solution)/shard_map/jit(_where)/select_n | solution.py:97
  223.1 7.2 %collective-permute-start.2 = (f32[4,4,256]{2,1,0:T(4,128)S(1)}, f32[4,4,256]{2,1,0:T(4,128)S(1)}, u32[]{:S(2)}, u32[]{:S(2)}) collective-permute-start(f32[4,4,256]{2,1,0:T(4,128)S(1)} %fusion.37), channel_id=1, source_target_pairs={{0,16},{16,32},{32,48},{48,64},{64,80},{80,96},{96,112},{112,128},... | collective-permute-start | bytes 49160 | tf_op jit(solution)/shard_map/ppermute | solution.py:24
  230.3 1.9 collective-permute-start.3
  232.7 6.6 %collective-permute-done.3 = f32[4,4,256]{2,1,0:T(4,128)S(1)} collective-permute-done((f32[4,4,256]{2,1,0:T(4,128)S(1)}, f32[4,4,256]{2,1,0:T(4,128)S(1)}, u32[]{:S(2)}, u32[]{:S(2)}) %collective-permute-start.3) | collective-permute-done | bytes 16416 | tf_op jit(solution)/shard_map/ppermute | solution.py:26
  240.4 1.9 collective-permute-start.6
  242.3 2.4 collective-permute-start.7
  245.4 3.1 collective-permute-done.7
  249.5 1.9 collective-permute-start.8
  251.4 104.3 %collective-permute-start.9 = (f32[4,4,256]{2,1,0:T(4,128)S(1)}, f32[4,4,256]{2,1,0:T(4,128)S(1)}, u32[]{:S(2)}, u32[]{:S(2)}) collective-permute-start(f32[4,4,256]{2,1,0:T(4,128)S(1)} %fusion.35), channel_id=1, source_target_pairs={{16,0},{32,16},{48,32},{64,48},{80,64},{96,80},{112,96},{128,112},... | collective-permute-start | bytes 49160 | tf_op jit(solution)/shard_map/ppermute | solution.py:26
  355.7 1.4 collective-permute-done.9
  358.2 1.9 collective-permute-start.10
  360.1 2.4 collective-permute-start.11
  363.2 3.1 collective-permute-done.11
  367.3 12.3 %collective-permute-start.12 = (f32[4,4,256]{2,1,0:T(4,128)S(1)}, f32[4,4,256]{2,1,0:T(4,128)S(1)}, u32[]{:S(2)}, u32[]{:S(2)}) collective-permute-start(f32[4,4,256]{2,1,0:T(4,128)S(1)} %fusion.33), channel_id=1, source_target_pairs={{0,16},{16,32},{32,48},{48,64},{64,80},{80,96},{96,112},{112,128},... | collective-permute-start | bytes 49160 | tf_op jit(solution)/shard_map/ppermute | solution.py:24
  379.5 1.9 collective-permute-start.13
  381.5 7.0 %collective-permute-done.13 = f32[4,4,256]{2,1,0:T(4,128)S(1)} collective-permute-done((f32[4,4,256]{2,1,0:T(4,128)S(1)}, f32[4,4,256]{2,1,0:T(4,128)S(1)}, u32[]{:S(2)}, u32[]{:S(2)}) %collective-permute-start.13) | collective-permute-done | bytes 16416 | tf_op jit(solution)/shard_map/ppermute | solution.py:26
  (143 shorter events, 32.0 us)
Async XLA Ops:
  0.6 47.1 %copy-start = (f32[8,4]{0,1:T(4,128)S(1)}, f32[8,4]{0,1:T(4,128)}, u32[]{:S(2)}) copy-start(f32[8,4]{0,1:T(4,128)} %param.20) | copy-start | bytes 388
  0.6 47.3 %copy-start.2 = (f32[8,8,4096]{2,1,0:T(8,128)S(1)}, f32[8,8,4096]{2,1,0:T(8,128)}, u32[]{:S(2)}) copy-start(f32[8,8,4096]{2,1,0:T(8,128)} %param.13) | copy-start | bytes 3145732
  0.7 47.3 %copy-start.6 = (f32[8,8]{1,0:T(8,128)S(1)}, f32[8,8]{1,0:T(8,128)}, u32[]{:S(2)}) copy-start(f32[8,8]{1,0:T(8,128)} %param.19) | copy-start | bytes 772
  1.7 219.8 %collective-permute-start.4 = (f32[1,1,256]{2,1,0:T(1,128)S(1)}, f32[1,1,256]{2,1,0:T(1,128)S(1)}, u32[]{:S(2)}, u32[]{:S(2)}) collective-permute-start(f32[1,1,256]{2,1,0:T(1,128)S(1)} %convolution_bitcast_fusion.4), channel_id=1, source_target_pairs={{0,16},{16,32},{32,48},{48,64},{64,80},{80,96},{96,112},{112,128},... | collective-permute-start | bytes 3080 | tf_op jit(solution)/shard_map/ppermute | solution.py:24
  7.1 214.3 %collective-permute-start.5 = (f32[1,1,256]{2,1,0:T(1,128)S(1)}, f32[1,1,256]{2,1,0:T(1,128)S(1)}, u32[]{:S(2)}, u32[]{:S(2)}) collective-permute-start(f32[1,1,256]{2,1,0:T(1,128)S(1)} %convolution_bitcast_fusion.4), channel_id=1, source_target_pairs={{16,0},{32,16},{48,32},{64,48},{80,64},{96,80},{112,96},{128,112},... | collective-permute-start | bytes 3080 | tf_op jit(solution)/shard_map/ppermute | solution.py:26
  9.9 212.1 %collective-permute-start = (f32[4,1,512]{2,1,0:T(1,128)S(1)}, f32[4,1,512]{2,1,0:T(1,128)S(1)}, u32[]{:S(2)}, u32[]{:S(2)}) collective-permute-start(f32[4,1,512]{2,1,0:T(1,128)S(1)} %get-tuple-element.121), channel_id=1, source_target_pairs={{1,0},{2,1},{3,2},{4,3},{5,4},{6,5},{7,6},{8,7},{9,8},{10,9},{11,1... | collective-permute-start | bytes 24584 | tf_op jit(solution)/shard_map/ppermute | solution.py:26
  11.8 210.2 %collective-permute-start.1 = (f32[4,1,512]{2,1,0:T(1,128)S(1)}, f32[4,1,512]{2,1,0:T(1,128)S(1)}, u32[]{:S(2)}, u32[]{:S(2)}) collective-permute-start(f32[4,1,512]{2,1,0:T(1,128)S(1)} %get-tuple-element.122), channel_id=1, source_target_pairs={{0,1},{1,2},{2,3},{3,4},{4,5},{5,6},{6,7},{7,8},{8,9},{9,10},{10,1... | collective-permute-start | bytes 24584 | tf_op jit(solution)/shard_map/ppermute | solution.py:24
  116.7 4.0 %copy-start.1 = (f32[8,8,4096]{2,1,0:T(8,128)}, f32[8,8,4096]{2,1,0:T(8,128)S(1)}, u32[]{:S(2)}) copy-start(f32[8,8,4096]{2,1,0:T(8,128)S(1)} %get-tuple-element.80) | copy-start | bytes 3145732
  120.7 19.9 %copy-start.9 = (f32[4,8]{1,0:T(4,128)S(1)}, f32[4,8]{1,0:T(4,128)}, u32[]{:S(2)}) copy-start(f32[4,8]{1,0:T(4,128)} %param.21) | copy-start | bytes 388
  120.7 20.4 %copy-start.8 = (f32[2,4,512]{2,1,0:T(4,128)S(1)}, f32[2,4,512]{2,1,0:T(4,128)}, u32[]{:S(2)}) copy-start(f32[2,4,512]{2,1,0:T(4,128)} %param.17) | copy-start | bytes 49156
  120.7 20.4 %copy-start.4 = (f32[512,512,1]{1,0,2:T(8,128)S(1)}, f32[512,512,1]{1,0,2:T(8,128)}, u32[]{:S(2)}) copy-start(f32[512,512,1]{1,0,2:T(8,128)} %constant.378) | copy-start | bytes 3145732
  120.8 20.4 %copy-start.5 = (f32[4,4,512]{2,1,0:T(4,128)S(1)}, f32[4,4,512]{2,1,0:T(4,128)}, u32[]{:S(2)}) copy-start(f32[4,4,512]{2,1,0:T(4,128)} %param.16) | copy-start | bytes 98308
  123.1 98.9 %copy-start.7 = (f32[512]{0:T(512)S(1)}, f32[512]{0:T(512)}, u32[]{:S(2)}) copy-start(f32[512]{0:T(512)} %param.18) | copy-start | bytes 6148
  123.1 99.0 %copy-start.3 = (f32[512,512,1]{1,0,2:T(8,128)S(1)}, f32[512,512,1]{1,0,2:T(8,128)}, u32[]{:S(2)}) copy-start(f32[512,512,1]{1,0,2:T(8,128)} %constant.379) | copy-start | bytes 3145732
  223.1 9.6 %collective-permute-start.2 = (f32[4,4,256]{2,1,0:T(4,128)S(1)}, f32[4,4,256]{2,1,0:T(4,128)S(1)}, u32[]{:S(2)}, u32[]{:S(2)}) collective-permute-start(f32[4,4,256]{2,1,0:T(4,128)S(1)} %fusion.37), channel_id=1, source_target_pairs={{0,16},{16,32},{32,48},{48,64},{64,80},{80,96},{96,112},{112,128},... | collective-permute-start | bytes 49160 | tf_op jit(solution)/shard_map/ppermute | solution.py:24
  230.3 9.0 %collective-permute-start.3 = (f32[4,4,256]{2,1,0:T(4,128)S(1)}, f32[4,4,256]{2,1,0:T(4,128)S(1)}, u32[]{:S(2)}, u32[]{:S(2)}) collective-permute-start(f32[4,4,256]{2,1,0:T(4,128)S(1)} %fusion.37), channel_id=1, source_target_pairs={{16,0},{32,16},{48,32},{64,48},{80,64},{96,80},{112,96},{128,112},... | collective-permute-start | bytes 49160 | tf_op jit(solution)/shard_map/ppermute | solution.py:26
  240.4 5.0 %collective-permute-start.6 = (f32[4,1,512]{2,1,0:T(1,128)S(1)}, f32[4,1,512]{2,1,0:T(1,128)S(1)}, u32[]{:S(2)}, u32[]{:S(2)}) collective-permute-start(f32[4,1,512]{2,1,0:T(1,128)S(1)} %get-tuple-element.119), channel_id=1, source_target_pairs={{1,0},{2,1},{3,2},{4,3},{5,4},{6,5},{7,6},{8,7},{9,8},{10,9},{11,1... | collective-permute-start | bytes 24584 | tf_op jit(solution)/shard_map/ppermute | solution.py:26
  242.3 6.2 %collective-permute-start.7 = (f32[4,1,512]{2,1,0:T(1,128)S(1)}, f32[4,1,512]{2,1,0:T(1,128)S(1)}, u32[]{:S(2)}, u32[]{:S(2)}) collective-permute-start(f32[4,1,512]{2,1,0:T(1,128)S(1)} %get-tuple-element.120), channel_id=1, source_target_pairs={{0,1},{1,2},{2,3},{3,4},{4,5},{5,6},{6,7},{7,8},{8,9},{9,10},{10,1... | collective-permute-start | bytes 24584 | tf_op jit(solution)/shard_map/ppermute | solution.py:24
  249.5 106.2 %collective-permute-start.8 = (f32[4,4,256]{2,1,0:T(4,128)S(1)}, f32[4,4,256]{2,1,0:T(4,128)S(1)}, u32[]{:S(2)}, u32[]{:S(2)}) collective-permute-start(f32[4,4,256]{2,1,0:T(4,128)S(1)} %fusion.35), channel_id=1, source_target_pairs={{0,16},{16,32},{32,48},{48,64},{64,80},{80,96},{96,112},{112,128},... | collective-permute-start | bytes 49160 | tf_op jit(solution)/shard_map/ppermute | solution.py:24
  251.4 105.7 %collective-permute-start.9 = (f32[4,4,256]{2,1,0:T(4,128)S(1)}, f32[4,4,256]{2,1,0:T(4,128)S(1)}, u32[]{:S(2)}, u32[]{:S(2)}) collective-permute-start(f32[4,4,256]{2,1,0:T(4,128)S(1)} %fusion.35), channel_id=1, source_target_pairs={{16,0},{32,16},{48,32},{64,48},{80,64},{96,80},{112,96},{128,112},... | collective-permute-start | bytes 49160 | tf_op jit(solution)/shard_map/ppermute | solution.py:26
  358.2 5.0 %collective-permute-start.10 = (f32[4,1,512]{2,1,0:T(1,128)S(1)}, f32[4,1,512]{2,1,0:T(1,128)S(1)}, u32[]{:S(2)}, u32[]{:S(2)}) collective-permute-start(f32[4,1,512]{2,1,0:T(1,128)S(1)} %get-tuple-element.117), channel_id=1, source_target_pairs={{1,0},{2,1},{3,2},{4,3},{5,4},{6,5},{7,6},{8,7},{9,8},{10,9},{11,1... | collective-permute-start | bytes 24584 | tf_op jit(solution)/shard_map/ppermute | solution.py:26
  360.1 6.2 %collective-permute-start.11 = (f32[4,1,512]{2,1,0:T(1,128)S(1)}, f32[4,1,512]{2,1,0:T(1,128)S(1)}, u32[]{:S(2)}, u32[]{:S(2)}) collective-permute-start(f32[4,1,512]{2,1,0:T(1,128)S(1)} %get-tuple-element.118), channel_id=1, source_target_pairs={{0,1},{1,2},{2,3},{3,4},{4,5},{5,6},{6,7},{7,8},{8,9},{9,10},{10,1... | collective-permute-start | bytes 24584 | tf_op jit(solution)/shard_map/ppermute | solution.py:24
  367.3 14.2 %collective-permute-start.12 = (f32[4,4,256]{2,1,0:T(4,128)S(1)}, f32[4,4,256]{2,1,0:T(4,128)S(1)}, u32[]{:S(2)}, u32[]{:S(2)}) collective-permute-start(f32[4,4,256]{2,1,0:T(4,128)S(1)} %fusion.33), channel_id=1, source_target_pairs={{0,16},{16,32},{32,48},{48,64},{64,80},{80,96},{96,112},{112,128},... | collective-permute-start | bytes 49160 | tf_op jit(solution)/shard_map/ppermute | solution.py:24
  379.5 9.0 %collective-permute-start.13 = (f32[4,4,256]{2,1,0:T(4,128)S(1)}, f32[4,4,256]{2,1,0:T(4,128)S(1)}, u32[]{:S(2)}, u32[]{:S(2)}) collective-permute-start(f32[4,4,256]{2,1,0:T(4,128)S(1)} %fusion.33), channel_id=1, source_target_pairs={{16,0},{32,16},{48,32},{64,48},{80,64},{96,80},{112,96},{128,112},... | collective-permute-start | bytes 49160 | tf_op jit(solution)/shard_map/ppermute | solution.py:26
where the time goes:
time: 393 us; the launch traced here: 390 us
  starting transfers between devices  150 us (38%)
  other arithmetic  93.6 us (24%)
  local copies, waits for them, and re-layouts  56.8 us (14%)
  blocking collectives  32.4 us (8%)
  matrix products  29.9 us (8%)
  waiting for transfers between devices  21.2 us (5%)
  loops' own time  5.2 us (1%)
    ppermute x7, starting transfers between devices, padded_2(): lax.ppermute(head, axis, [((i + 1) % count, i) for i in range(ends)])  116 us
    ppermute x7, starting transfers between devices, padded_2(): lax.ppermute(tail, axis, [(i, (i + 1) % count) for i in range(ends)])  34.1 us
    select_n x1, other arithmetic, edge_tables(): jnp.where(col_of == 0, left_source, jnp.where(col_of == 3, right_source,...  31.2 us
    select_n x1, other arithmetic, edge_tables(): jnp.where(row_of == 0, lower_source, jnp.where(row_of == 3, upper_source,...  30.8 us
    dot_general x6, matrix products, one_step(): jnp.einsum('gf,nfc->ngc', coupling, current, precision=highest)  19 us
    all_gather x1, blocking collectives, shards(): every_change = lax.all_gather(change, 'lev', axis=0, tiled=True)  17.1 us
    all_gather x1, blocking collectives, shards(): every_host = lax.all_gather(host_columns, 'lev', axis=2, tiled=True)  15.3 us
    ppermute x7, waiting for transfers between devices, padded_2(): lax.ppermute(head, axis, [((i + 1) % count, i) for i in range(ends)])  15 us
  transfers between devices with their start and end apart: 14, of which 5 were waited for; matrix products, arithmetic and copies ran while one was open for 44% of the time, Pallas kernels for 0%

commit v1 on v0

--- a/solution.py
+++ b/solution.py
@@ -156,7 +156,9 @@
     change = (
         (cloud_new - cloud_state).reshape(own_rows, n_fields, n_levels, cell_width).mean(axis=3)
     )
-    every_change = lax.all_gather(change, "lev", axis=0, tiled=True)
+    every_change = jnp.concatenate(
+        lax.all_to_all(jnp.stack([change] * lax.axis_size("lev")), "lev", 0, 0), axis=0
+    )
     level_change = lax.dynamic_slice_in_dim(every_change, lev_at * lev_dev, lev_dev, 2)
     column_tendency = jnp.einsum("vf,nfl->vln", feedback_map, level_change, precision=highest)
     physics = jnp.dot(

time: 393 us -> 378 us (0.962)
  blocking collectives: 32.4 us -> 15.1 us
  local copies, waits for them, and re-layouts: 56.8 us -> 48.4 us
  starting transfers between devices: 150 us -> 158 us
    all_gather x1 -> x0, blocking collectives: 17.1 us -> none  [shards(): every_change = lax.all_gather(change, 'lev', axis=0, tiled=True)]
    all_to_all x0 -> x1, starting transfers between devices: none -> 7.22 us  [shards(): lax.all_to_all(jnp.stack([change] * lax.axis_size('lev')), 'lev', 0, 0)]
    gather x4, local copies, waits for them, and re-layouts: 8.41 us -> 2.9 us  [edge_tables(): lower_ids = element_links[:, 2][elem_of] % elem_dev]
  transfers between devices with their start and end apart: 14 -> 15, of which waited for: 5 -> 5; matrix products, arithmetic and copies ran while one was open for 44% -> 44% of each run, Pallas kernels for 0% -> 0%
where the time goes in v1:
time: 378 us; the launch traced here: 375 us
  starting transfers between devices  158 us (42%)
  other arithmetic  95.3 us (25%)
  local copies, waits for them, and re-layouts  48.4 us (13%)
  matrix products  29.9 us (8%)
  waiting for transfers between devices  21.7 us (6%)
  blocking collectives  15.1 us (4%)
  loops' own time  5.2 us (1%)
    ppermute x7, starting transfers between devices, padded_2(): lax.ppermute(head, axis, [((i + 1) % count, i) for i in range(ends)])  118 us
    ppermute x7, starting transfers between devices, padded_2(): lax.ppermute(tail, axis, [(i, (i + 1) % count) for i in range(ends)])  33.2 us
    select_n x1, other arithmetic, edge_tables(): jnp.where(col_of == 0, left_source, jnp.where(col_of == 3, right_source,...  31.2 us
    select_n x1, other arithmetic, edge_tables(): jnp.where(row_of == 0, lower_source, jnp.where(row_of == 3, upper_source,...  31.1 us
    dot_general x6, matrix products, one_step(): jnp.einsum('gf,nfc->ngc', coupling, current, precision=highest)  19 us
    all_gather x1, blocking collectives, shards(): every_host = lax.all_gather(host_columns, 'lev', axis=2, tiled=True)  15.1 us
    ppermute x7, waiting for transfers between devices, padded_2(): lax.ppermute(head, axis, [((i + 1) % count, i) for i in range(ends)])  15 us
    add x6, local copies, waits for them, and re-layouts, one_step(): eastward + westward - 2.0 * current  9.86 us
  transfers between devices with their start and end apart: 15, of which 5 were waited for; matrix products, arithmetic and copies ran while one was open for 44% of the time, Pallas kernels for 0%

profile of v1, /device:TPU:230, one launch (start us, length us, event | category | flops | bytes accessed | tf_op | source)
XLA Modules:
  0.0 375.3 jit_solution(9304141950277809093)
XLA Ops:
  0.7 1.0 convolution_bitcast_fusion.4
  1.7 5.4 %collective-permute-start.4 = (f32[1,1,256]{2,1,0:T(1,128)S(1)}, f32[1,1,256]{2,1,0:T(1,128)S(1)}, u32[]{:S(2)}, u32[]{:S(2)}) collective-permute-start(f32[1,1,256]{2,1,0:T(1,128)S(1)} %convolution_bitcast_fusion.4), channel_id=1, source_target_pairs={{0,16},{16,32},{32,48},{48,64},{64,80},{80,96},{96,112},{112,128},... | collective-permute-start | bytes 3080 | tf_op jit(solution)/shard_map/ppermute | solution.py:24
  7.1 1.9 collective-permute-start.5
  10.2 15.1 %all_gather.3 = f32[128,4,64]{0,1,2:T(4,128)S(1)} all-gather(f32[128,4,4]{0,1,2:T(4,128)S(1)} %bitcast.240), channel_id=1, replica_groups=mesh['elem'=32,'lev'=16] {'lev'}, dimensions={2}, use_global_device_ids=true | all-gather | bytes 139264 | tf_op jit(solution)/shard_map/all_gather | solution.py:150
  25.6 1.5 fusion.127
  27.3 68.8 %while.13 = (s32[]{:T(128)}, f32[8,8,4096]{2,1,0:T(8,128)S(1)}, s32[]{:T(128)}, s32[8]{0:T(128)S(1)}, f32[8,8]{1,0:T(8,128)S(1)}, /*index=5*/f32[8,8,64]{2,1,0:T(8,128)S(1)}, s32[]{:T(128)}) while((s32[]{:T(128)}, f32[8,8,4096]{2,1,0:T(8,128)S(1)}, s32[]{:T(128)}, s32[8]{0:T(128)S(1)}, f32[8,8]{1,0:T(8,128)S(1)}, ...), condition=%wide.region_2.3_spmd.clone, body=%wide.region_1.2_spmd.clone.sunk | while | flops 28835848 | bytes 22041208 | solution.py:76
  28.1 0.8 reshape.1006
  30.4 1.2 maximum_add_fusion.2
  31.6 1.6 add.881
  33.8 1.6 reshape.1005
  35.5 3.2 fusion.176
  39.4 0.8 reshape.1006
  41.8 1.2 maximum_add_fusion.2
  42.9 1.6 add.881
  45.2 1.6 reshape.1005
  46.8 3.2 fusion.176
  53.1 1.2 maximum_add_fusion.2
  54.3 1.6 add.881
  56.5 1.6 reshape.1005
  58.1 3.2 fusion.176
  62.1 0.8 reshape.1006
  64.4 1.2 maximum_add_fusion.2
  65.6 1.6 add.881
  67.9 1.6 reshape.1005
  69.5 3.2 fusion.176
  73.4 0.8 reshape.1006
  75.8 1.2 maximum_add_fusion.2
  76.9 1.6 add.881
  79.2 1.6 reshape.1005
  80.8 3.2 fusion.176
  84.8 0.8 reshape.1006
  87.1 1.2 maximum_add_fusion.2
  88.3 1.6 add.881
  90.5 1.6 reshape.1005
  92.2 3.2 fusion.176
  96.1 1.8 sub.95
  97.9 2.2 reshape.408
  100.1 2.3 reduce_sum.9
  102.4 1.0 reshape.1001
  103.5 7.2 %all-to-all-start = ((f32[16,1,4096]{2,1,0:T(1,128)}), f32[16,1,4096]{2,1,0:T(1,128)S(1)}, u32[]{:S(2)}, u32[]{:S(2)}) async-start(f32[16,1,4096]{2,1,0:T(1,128)} %reshape.1001), calls=%async_computation | async-start | bytes 524288 | tf_op jit(solution)/shard_map/all_to_all | solution.py:160
  110.7 2.2 collective-permute-start
  112.9 2.3 collective-permute-start.1
  122.0 4.4 %select_select_fusion.3 = s32[512,1]{0,1:T(1,128)S(1)} fusion(s32[]{:T(128)} %bitcast.41, s32[]{:T(128)} %bitcast.42, s32[]{:T(128)} %bitcast.43, s32[]{:T(128)} %bitcast.44, s32[]{:T(128)} %bitcast.45, s32[]{:T(128)} %bitcast.47, s32[]{:T(128)} %bitcast.46), kind=kLoop, calls=%fused_computation.216 | loop fusion | flops 11776 | bytes 2076 | tf_op jit(solution)/shard_map/gather | solution.py:91
  126.4 4.5 %select_select_fusion.1 = s32[512,1]{0,1:T(1,128)S(1)} fusion(s32[]{:T(128)} %bitcast.107, s32[]{:T(128)} %bitcast.108, s32[]{:T(128)} %bitcast.109, s32[]{:T(128)} %bitcast.110, s32[]{:T(128)} %bitcast.111, s32[]{:T(128)} %bitcast.113, s32[]{:T(128)} %bitcast.112), kind=kLoop, calls=%fused_computation.214 | loop fusion | flops 11776 | bytes 2076 | tf_op jit(solution)/shard_map/gather | solution.py:101
  130.9 4.4 %select_select_fusion = s32[512,1]{0,1:T(1,128)S(1)} fusion(s32[]{:T(128)} %bitcast.140, s32[]{:T(128)} %bitcast.141, s32[]{:T(128)} %bitcast.142, s32[]{:T(128)} %bitcast.143, s32[]{:T(128)} %bitcast.144, s32[]{:T(128)} %bitcast.146, s32[]{:T(128)} %bitcast.145), kind=kLoop, calls=%fused_computation.213 | loop fusion | flops 11776 | bytes 2076 | tf_op jit(solution)/shard_map/gather | solution.py:102
  135.3 31.1 %fusion.104 = s32[512]{0:T(512)S(1)} fusion(pred[512]{0:T(512)(128)(4,1)S(1)} %compare_reduce_fusion, pred[512]{0:T(512)(128)(4,1)S(1)} %compare_reduce_fusion.1, pred[512]{0:T(512)(128)(4,1)S(1)} %compare_reduce_fusion.2, pred[512]{0:T(512)(128)(4,1)S(1)} %compare_reduce_fusion.3, pred[512]{0:T(512)(128)(4,1)S(1)} %compare_reduce_fusion.4, ...), kind=kLoop, calls=%fused_computation.204 | loop fusion | flops 53248 | bytes 19144 | tf_op jit(solution)/shard_map/jit(_where)/select_n | solution.py:105
  166.4 4.4 %select_select_fusion.2 = s32[512,1]{0,1:T(1,128)S(1)} fusion(s32[]{:T(128)} %bitcast.74, s32[]{:T(128)} %bitcast.75, s32[]{:T(128)} %bitcast.76, s32[]{:T(128)} %bitcast.77, s32[]{:T(128)} %bitcast.78, s32[]{:T(128)} %bitcast.80, s32[]{:T(128)} %bitcast.79), kind=kLoop, calls=%fused_computation.215 | loop fusion | flops 11776 | bytes 2076 | tf_op jit(solution)/shard_map/gather | solution.py:92
  170.8 31.2 %fusion.94 = s32[512]{0:T(512)S(1)} fusion(pred[512]{0:T(512)(128)(4,1)S(1)} %compare_reduce_fusion, pred[512]{0:T(512)(128)(4,1)S(1)} %compare_reduce_fusion.1, pred[512]{0:T(512)(128)(4,1)S(1)} %compare_reduce_fusion.2, pred[512]{0:T(512)(128)(4,1)S(1)} %compare_reduce_fusion.3, pred[512]{0:T(512)(128)(4,1)S(1)} %compare_reduce_fusion.4, ...), kind=kLoop, calls=%fused_computation.194 | loop fusion | flops 64512 | bytes 19148 | tf_op jit(solution)/shard_map/jit(_where)/select_n | solution.py:97
  203.1 1.3 reduce.50
  206.6 7.2 %collective-permute-start.2 = (f32[4,4,256]{2,1,0:T(4,128)S(1)}, f32[4,4,256]{2,1,0:T(4,128)S(1)}, u32[]{:S(2)}, u32[]{:S(2)}) collective-permute-start(f32[4,4,256]{2,1,0:T(4,128)S(1)} %fusion.37), channel_id=1, source_target_pairs={{0,16},{16,32},{32,48},{48,64},{64,80},{80,96},{96,112},{112,128},... | collective-permute-start | bytes 49160 | tf_op jit(solution)/shard_map/ppermute | solution.py:24
  213.9 1.9 collective-permute-start.3
  216.2 6.6 %collective-permute-done.3 = f32[4,4,256]{2,1,0:T(4,128)S(1)} collective-permute-done((f32[4,4,256]{2,1,0:T(4,128)S(1)}, f32[4,4,256]{2,1,0:T(4,128)S(1)}, u32[]{:S(2)}, u32[]{:S(2)}) %collective-permute-start.3) | collective-permute-done | bytes 16416 | tf_op jit(solution)/shard_map/ppermute | solution.py:26
  224.0 3.1 collective-permute-start.6
  227.1 1.9 collective-permute-start.7
  229.7 3.6 collective-permute-done.7
  234.3 1.9 collective-permute-start.8
  236.2 104.8 %collective-permute-start.9 = (f32[4,4,256]{2,1,0:T(4,128)S(1)}, f32[4,4,256]{2,1,0:T(4,128)S(1)}, u32[]{:S(2)}, u32[]{:S(2)}) collective-permute-start(f32[4,4,256]{2,1,0:T(4,128)S(1)} %fusion.35), channel_id=1, source_target_pairs={{16,0},{32,16},{48,32},{64,48},{80,64},{96,80},{112,96},{128,112},... | collective-permute-start | bytes 49160 | tf_op jit(solution)/shard_map/ppermute | solution.py:26
  341.1 1.4 collective-permute-done.9
  343.6 1.9 collective-permute-start.10
  345.5 2.4 collective-permute-start.11
  348.6 3.1 collective-permute-done.11
  352.6 12.0 %collective-permute-start.12 = (f32[4,4,256]{2,1,0:T(4,128)S(1)}, f32[4,4,256]{2,1,0:T(4,128)S(1)}, u32[]{:S(2)}, u32[]{:S(2)}) collective-permute-start(f32[4,4,256]{2,1,0:T(4,128)S(1)} %fusion.33), channel_id=1, source_target_pairs={{0,16},{16,32},{32,48},{48,64},{64,80},{80,96},{96,112},{112,128},... | collective-permute-start | bytes 49160 | tf_op jit(solution)/shard_map/ppermute | solution.py:24
  364.6 1.9 collective-permute-start.13
  366.6 7.0 %collective-permute-done.13 = f32[4,4,256]{2,1,0:T(4,128)S(1)} collective-permute-done((f32[4,4,256]{2,1,0:T(4,128)S(1)}, f32[4,4,256]{2,1,0:T(4,128)S(1)}, u32[]{:S(2)}, u32[]{:S(2)}) %collective-permute-start.13) | collective-permute-done | bytes 16416 | tf_op jit(solution)/shard_map/ppermute | solution.py:26
  (151 shorter events, 32.9 us)
Async XLA Ops:
  0.6 26.4 %copy-start = (f32[8,4]{0,1:T(4,128)S(1)}, f32[8,4]{0,1:T(4,128)}, u32[]{:S(2)}) copy-start(f32[8,4]{0,1:T(4,128)} %param.20) | copy-start | bytes 388
  0.6 26.6 %copy-start.2 = (f32[8,8,4096]{2,1,0:T(8,128)S(1)}, f32[8,8,4096]{2,1,0:T(8,128)}, u32[]{:S(2)}) copy-start(f32[8,8,4096]{2,1,0:T(8,128)} %param.13) | copy-start | bytes 3145732
  0.7 26.6 %copy-start.7 = (f32[8,8]{1,0:T(8,128)S(1)}, f32[8,8]{1,0:T(8,128)}, u32[]{:S(2)}) copy-start(f32[8,8]{1,0:T(8,128)} %param.19) | copy-start | bytes 772
  1.7 200.3 %collective-permute-start.4 = (f32[1,1,256]{2,1,0:T(1,128)S(1)}, f32[1,1,256]{2,1,0:T(1,128)S(1)}, u32[]{:S(2)}, u32[]{:S(2)}) collective-permute-start(f32[1,1,256]{2,1,0:T(1,128)S(1)} %convolution_bitcast_fusion.4), channel_id=1, source_target_pairs={{0,16},{16,32},{32,48},{48,64},{64,80},{80,96},{96,112},{112,128},... | collective-permute-start | bytes 3080 | tf_op jit(solution)/shard_map/ppermute | solution.py:24
  7.1 194.9 %collective-permute-start.5 = (f32[1,1,256]{2,1,0:T(1,128)S(1)}, f32[1,1,256]{2,1,0:T(1,128)S(1)}, u32[]{:S(2)}, u32[]{:S(2)}) collective-permute-start(f32[1,1,256]{2,1,0:T(1,128)S(1)} %convolution_bitcast_fusion.4), channel_id=1, source_target_pairs={{16,0},{32,16},{48,32},{64,48},{80,64},{96,80},{112,96},{128,112},... | collective-permute-start | bytes 3080 | tf_op jit(solution)/shard_map/ppermute | solution.py:26
  96.0 4.0 %copy-start.1 = (f32[8,8,4096]{2,1,0:T(8,128)}, f32[8,8,4096]{2,1,0:T(8,128)S(1)}, u32[]{:S(2)}) copy-start(f32[8,8,4096]{2,1,0:T(8,128)S(1)} %get-tuple-element.80) | copy-start | bytes 3145732
  100.0 10.6 %copy-start.6 = (f32[4,4,512]{2,1,0:T(4,128)S(1)}, f32[4,4,512]{2,1,0:T(4,128)}, u32[]{:S(2)}) copy-start(f32[4,4,512]{2,1,0:T(4,128)} %param.16) | copy-start | bytes 98308
  100.0 15.2 %copy-start.5 = (s32[32,4]{0,1:T(4,128)S(1)}, s32[32,4]{0,1:T(4,128)}, u32[]{:S(2)}) copy-start(s32[32,4]{0,1:T(4,128)} %param.15) | copy-start | bytes 1540
  100.0 21.1 %copy-start.9 = (f32[2,4,512]{2,1,0:T(4,128)S(1)}, f32[2,4,512]{2,1,0:T(4,128)}, u32[]{:S(2)}) copy-start(f32[2,4,512]{2,1,0:T(4,128)} %param.17) | copy-start | bytes 49156
  100.1 21.2 %copy-start.4 = (f32[512,512,1]{1,0,2:T(8,128)S(1)}, f32[512,512,1]{1,0,2:T(8,128)}, u32[]{:S(2)}) copy-start(f32[512,512,1]{1,0,2:T(8,128)} %constant.378) | copy-start | bytes 3145732
  102.4 100.2 %copy-start.8 = (f32[512]{0:T(512)S(1)}, f32[512]{0:T(512)}, u32[]{:S(2)}) copy-start(f32[512]{0:T(512)} %param.18) | copy-start | bytes 6148
  103.5 99.2 %all-to-all-start = ((f32[16,1,4096]{2,1,0:T(1,128)}), f32[16,1,4096]{2,1,0:T(1,128)S(1)}, u32[]{:S(2)}, u32[]{:S(2)}) async-start(f32[16,1,4096]{2,1,0:T(1,128)} %reshape.1001), calls=%async_computation | async-start | bytes 524288 | tf_op jit(solution)/shard_map/all_to_all | solution.py:160
  110.7 94.8 %collective-permute-start = (f32[4,1,512]{2,1,0:T(1,128)S(1)}, f32[4,1,512]{2,1,0:T(1,128)S(1)}, u32[]{:S(2)}, u32[]{:S(2)}) collective-permute-start(f32[4,1,512]{2,1,0:T(1,128)S(1)} %get-tuple-element.121), channel_id=1, source_target_pairs={{1,0},{2,1},{3,2},{4,3},{5,4},{6,5},{7,6},{8,7},{9,8},{10,9},{11,1... | collective-permute-start | bytes 24584 | tf_op jit(solution)/shard_map/ppermute | solution.py:26
  112.9 92.7 %collective-permute-start.1 = (f32[4,1,512]{2,1,0:T(1,128)S(1)}, f32[4,1,512]{2,1,0:T(1,128)S(1)}, u32[]{:S(2)}, u32[]{:S(2)}) collective-permute-start(f32[4,1,512]{2,1,0:T(1,128)S(1)} %get-tuple-element.122), channel_id=1, source_target_pairs={{0,1},{1,2},{2,3},{3,4},{4,5},{5,6},{6,7},{7,8},{8,9},{9,10},{10,1... | collective-permute-start | bytes 24584 | tf_op jit(solution)/shard_map/ppermute | solution.py:24
  122.0 83.1 %copy-start.10 = (f32[4,8]{1,0:T(4,128)S(1)}, f32[4,8]{1,0:T(4,128)}, u32[]{:S(2)}) copy-start(f32[4,8]{1,0:T(4,128)} %param.21) | copy-start | bytes 388
  122.0 83.6 %copy-start.3 = (f32[512,512,1]{1,0,2:T(8,128)S(1)}, f32[512,512,1]{1,0,2:T(8,128)}, u32[]{:S(2)}) copy-start(f32[512,512,1]{1,0,2:T(8,128)} %constant.379) | copy-start | bytes 3145732
  206.6 9.6 %collective-permute-start.2 = (f32[4,4,256]{2,1,0:T(4,128)S(1)}, f32[4,4,256]{2,1,0:T(4,128)S(1)}, u32[]{:S(2)}, u32[]{:S(2)}) collective-permute-start(f32[4,4,256]{2,1,0:T(4,128)S(1)} %fusion.37), channel_id=1, source_target_pairs={{0,16},{16,32},{32,48},{48,64},{64,80},{80,96},{96,112},{112,128},... | collective-permute-start | bytes 49160 | tf_op jit(solution)/shard_map/ppermute | solution.py:24
  213.9 9.0 %collective-permute-start.3 = (f32[4,4,256]{2,1,0:T(4,128)S(1)}, f32[4,4,256]{2,1,0:T(4,128)S(1)}, u32[]{:S(2)}, u32[]{:S(2)}) collective-permute-start(f32[4,4,256]{2,1,0:T(4,128)S(1)} %fusion.37), channel_id=1, source_target_pairs={{16,0},{32,16},{48,32},{64,48},{80,64},{96,80},{112,96},{128,112},... | collective-permute-start | bytes 49160 | tf_op jit(solution)/shard_map/ppermute | solution.py:26
  224.0 5.7 %collective-permute-start.6 = (f32[4,1,512]{2,1,0:T(1,128)S(1)}, f32[4,1,512]{2,1,0:T(1,128)S(1)}, u32[]{:S(2)}, u32[]{:S(2)}) collective-permute-start(f32[4,1,512]{2,1,0:T(1,128)S(1)} %get-tuple-element.119), channel_id=1, source_target_pairs={{1,0},{2,1},{3,2},{4,3},{5,4},{6,5},{7,6},{8,7},{9,8},{10,9},{11,1... | collective-permute-start | bytes 24584 | tf_op jit(solution)/shard_map/ppermute | solution.py:26
  227.1 6.2 %collective-permute-start.7 = (f32[4,1,512]{2,1,0:T(1,128)S(1)}, f32[4,1,512]{2,1,0:T(1,128)S(1)}, u32[]{:S(2)}, u32[]{:S(2)}) collective-permute-start(f32[4,1,512]{2,1,0:T(1,128)S(1)} %get-tuple-element.120), channel_id=1, source_target_pairs={{0,1},{1,2},{2,3},{3,4},{4,5},{5,6},{6,7},{7,8},{8,9},{9,10},{10,1... | collective-permute-start | bytes 24584 | tf_op jit(solution)/shard_map/ppermute | solution.py:24
  234.3 106.8 %collective-permute-start.8 = (f32[4,4,256]{2,1,0:T(4,128)S(1)}, f32[4,4,256]{2,1,0:T(4,128)S(1)}, u32[]{:S(2)}, u32[]{:S(2)}) collective-permute-start(f32[4,4,256]{2,1,0:T(4,128)S(1)} %fusion.35), channel_id=1, source_target_pairs={{0,16},{16,32},{32,48},{48,64},{64,80},{80,96},{96,112},{112,128},... | collective-permute-start | bytes 49160 | tf_op jit(solution)/shard_map/ppermute | solution.py:24
  236.2 106.3 %collective-permute-start.9 = (f32[4,4,256]{2,1,0:T(4,128)S(1)}, f32[4,4,256]{2,1,0:T(4,128)S(1)}, u32[]{:S(2)}, u32[]{:S(2)}) collective-permute-start(f32[4,4,256]{2,1,0:T(4,128)S(1)} %fusion.35), channel_id=1, source_target_pairs={{16,0},{32,16},{48,32},{64,48},{80,64},{96,80},{112,96},{128,112},... | collective-permute-start | bytes 49160 | tf_op jit(solution)/shard_map/ppermute | solution.py:26
  343.6 5.0 %collective-permute-start.10 = (f32[4,1,512]{2,1,0:T(1,128)S(1)}, f32[4,1,512]{2,1,0:T(1,128)S(1)}, u32[]{:S(2)}, u32[]{:S(2)}) collective-permute-start(f32[4,1,512]{2,1,0:T(1,128)S(1)} %get-tuple-element.117), channel_id=1, source_target_pairs={{1,0},{2,1},{3,2},{4,3},{5,4},{6,5},{7,6},{8,7},{9,8},{10,9},{11,1... | collective-permute-start | bytes 24584 | tf_op jit(solution)/shard_map/ppermute | solution.py:26
  345.5 6.2 %collective-permute-start.11 = (f32[4,1,512]{2,1,0:T(1,128)S(1)}, f32[4,1,512]{2,1,0:T(1,128)S(1)}, u32[]{:S(2)}, u32[]{:S(2)}) collective-permute-start(f32[4,1,512]{2,1,0:T(1,128)S(1)} %get-tuple-element.118), channel_id=1, source_target_pairs={{0,1},{1,2},{2,3},{3,4},{4,5},{5,6},{6,7},{7,8},{8,9},{9,10},{10,1... | collective-permute-start | bytes 24584 | tf_op jit(solution)/shard_map/ppermute | solution.py:24
  352.6 13.9 %collective-permute-start.12 = (f32[4,4,256]{2,1,0:T(4,128)S(1)}, f32[4,4,256]{2,1,0:T(4,128)S(1)}, u32[]{:S(2)}, u32[]{:S(2)}) collective-permute-start(f32[4,4,256]{2,1,0:T(4,128)S(1)} %fusion.33), channel_id=1, source_target_pairs={{0,16},{16,32},{32,48},{48,64},{64,80},{80,96},{96,112},{112,128},... | collective-permute-start | bytes 49160 | tf_op jit(solution)/shard_map/ppermute | solution.py:24
  364.6 9.0 %collective-permute-start.13 = (f32[4,4,256]{2,1,0:T(4,128)S(1)}, f32[4,4,256]{2,1,0:T(4,128)S(1)}, u32[]{:S(2)}, u32[]{:S(2)}) collective-permute-start(f32[4,4,256]{2,1,0:T(4,128)S(1)} %fusion.33), channel_id=1, source_target_pairs={{16,0},{32,16},{48,32},{64,48},{80,64},{96,80},{112,96},{128,112},... | collective-permute-start | bytes 49160 | tf_op jit(solution)/shard_map/ppermute | solution.py:26
